TPU v7x, 32 devices: a whole 2x2x4 slice. The times are simulated.
32 devices in a mesh: grp: 2 (over y), tm: 16 (over z, x, core).
Axes of the slice: x: 2, y: 2, z: 4, core: 2. Of those that a mesh axis runs over, the one named last changes fastest.
Arguments:
- traces: float32 [2048, 16384], P('grp', 'tm'), parts along dimension 0, may hold values from -6 to 6
- templates: float32 [64, 8192], P('tm'), may hold values from -6 to 6
- moveouts: int32 [2048], P('grp'), parts along dimension 0, may hold values from 0 to 2047
- masks: int32 [64, 2048], P(None, 'grp'), parts along dimension 1, may hold values 0 or 1
Outputs:
- detection: float32 [64, 16384], P('tm', 'grp'), parts along dimension 1
There are 2 independent parts, one for each index of `grp`. A program takes and returns all parts, laid end to end along the dimension named above; an argument that names none is the same for every part. Nothing has to cross between parts.
All inputs are finite; a program needn't handle non-finite values.
Results may differ from a plain program's by a relative error of at most 0.000073.
Values sent between devices are 32-bit elements; how exact they have to be, the bound alone decides.
A program may use at most 64 MiB of HBM per device.

v0:
```python
import functools
import math

import jax
import jax.numpy as jnp
import numpy as np
from jax import lax
from jax.experimental import pallas as pl
from jax.experimental.pallas import tpu as pltpu
from jax.sharding import PartitionSpec as P

f32, bf16 = jnp.float32, jnp.bfloat16
LANES = 128
REACH = 2048


def split(value):
    high = value.astype(bf16)
    return high, (value - high.astype(f32)).astype(bf16)


def split_table(table):
    high = table.astype(jnp.bfloat16)
    return high, (table - high.astype(np.float64)).astype(jnp.bfloat16)


def transform(rows, first_ref, forward_ref, cosine, sine):
    outer = cosine.shape[0]
    high, low = split(jnp.concatenate(rows, axis=1))
    first = jnp.dot(first_ref[...], jnp.concatenate([high, high, low], axis=0), preferred_element_type=f32)
    turned = []
    for r in range(len(rows)):
        re = first[:outer, r * LANES : (r + 1) * LANES]
        im = first[outer:, r * LANES : (r + 1) * LANES]
        turned.append(jnp.concatenate([re * cosine + im * sine, im * cosine - re * sine], axis=1))
    high, low = split(jnp.concatenate(turned, axis=0))
    return jnp.dot(jnp.concatenate([high, low, high], axis=1), forward_ref[...], preferred_element_type=f32)


def shift(traces_ref, late, terms, base, group, channels):
    rows = 16
    blocks = traces_ref.shape[1] // LANES
    window = blocks + REACH // LANES
    here = pl.ds(pl.multiple_of(group * rows, rows), rows)
    delay = late[here, :]
    lane = lax.broadcasted_iota(jnp.int32, (rows, LANES), 1)
    inner = (delay & (LANES - 1)) + 1
    index = (lane - inner) & (LANES - 1)
    keep = lane >= inner
    turned = [
        jnp.take_along_axis(
            traces_ref[here, b * LANES : (b + 1) * LANES], index, axis=1, mode="promise_in_bounds"
        )
        for b in range(blocks)
    ]
    zero = jnp.zeros((rows, LANES), f32)
    moved = [
        jnp.where(keep, turned[b] if b < blocks else zero, turned[b - 1] if b > 0 else zero)
        for b in range(blocks + 1)
    ]
    hop = 1
    while hop < REACH // LANES:
        chosen = ((delay // LANES) & hop) != 0
        moved = [
            jnp.where(
                chosen,
                moved[b - hop] if b >= hop else zero,
                moved[b] if b < len(moved) else zero,
            )
            for b in range(len(moved) + hop)
        ]
        hop *= 2
    for b in range(window):
        high, low = split(moved[b])
        column = slice(b * LANES, (b + 1) * LANES)
        terms[pl.ds(pl.multiple_of(base + group * rows, rows), rows), column] = high
        terms[pl.ds(pl.multiple_of(channels + base + group * rows, rows), rows), column] = low


def kernel(
    devices,
    channels,
    moveout_ref,
    traces_ref,
    mask_hbm,
    template_hbm,
    first_hbm,
    forward_hbm,
    back_hbm,
    last_hbm,
    twiddle_hbm,
    out_ref,
    mask_ref,
    template_ref,
    first_ref,
    forward_ref,
    back_ref,
    last_ref,
    twiddle_ref,
    late,
    terms,
    part,
    arrived,
    merged,
    joined,
    series,
    tail,
    load_sem,
    pair_send,
    pair_recv,
    send_sem,
    recv_sem,
):
    step = pl.program_id(0)
    steps = pl.num_programs(0)
    depth, width = traces_ref.shape
    each, lags = template_ref.shape
    pairs = devices // 2
    me = lax.axis_index("tm")
    core = lax.rem(me, 2)
    pair = me // 2
    partner = me + 1 - 2 * core
    blocks = width // LANES
    window = blocks + REACH // LANES
    outer = devices * blocks
    loads = [
        pltpu.make_async_copy(source, target, load_sem.at[i])
        for i, (source, target) in enumerate(
            (
                (mask_hbm, mask_ref),
                (template_hbm, template_ref),
                (first_hbm, first_ref),
                (forward_hbm, forward_ref),
                (twiddle_hbm, twiddle_ref),
                (back_hbm, back_ref),
                (last_hbm, last_ref),
            )
        )
    ]
    barrier = pltpu.get_barrier_semaphore()

    @pl.when(step == 0)
    def _():
        for load in loads:
            load.start()

        def greet(i, _):
            target = 2 * lax.rem(pair + i, pairs) + core
            pl.semaphore_signal(barrier, inc=1, device_id={"tm": target}, device_id_type=pl.DeviceIdType.MESH)
            return 0

        pl.semaphore_signal(barrier, inc=1, device_id={"tm": partner}, device_id_type=pl.DeviceIdType.MESH)
        lax.fori_loop(1, pairs, greet, 0)

    for piece in range(depth // LANES):
        row = (REACH - 1) - moveout_ref[:, piece * LANES : (piece + 1) * LANES]
        late[piece * LANES : (piece + 1) * LANES, :] = jnp.broadcast_to(row, (LANES, LANES)).T

    def group_pair(i, _):
        for k in range(2):
            shift(traces_ref, late, terms, step * depth, 2 * i + k, channels)
        return 0

    lax.fori_loop(0, depth // 32, group_pair, 0)

    def far(k):
        near = (k + 1) // 2
        return lax.rem(pair + pairs // 2 + near * (1 - 2 * lax.rem(k, 2)), pairs)

    def to_partner(g):
        return pltpu.make_async_remote_copy(
            src_ref=part.at[1 - core, g],
            dst_ref=arrived.at[g],
            send_sem=pair_send.at[g],
            recv_sem=pair_recv.at[g],
            device_id={"tm": partner},
            device_id_type=pl.DeviceIdType.MESH,
        )

    def to_owner(k):
        g = far(k)
        return pltpu.make_async_remote_copy(
            src_ref=merged.at[g],
            dst_ref=joined.at[pair],
            send_sem=send_sem.at[k],
            recv_sem=recv_sem.at[k],
            device_id={"tm": 2 * g + core},
            device_id_type=pl.DeviceIdType.MESH,
        )

    @pl.when(step == steps - 1)
    def _():
        loads[0].wait()
        mask = mask_ref[...].astype(f32).astype(bf16)
        double = jnp.concatenate([mask, mask], axis=1)
        span = 2 if window % 2 == 0 else 1
        for b in range(0, window, span):
            added = jnp.dot(double, terms[:, b * LANES : (b + span) * LANES], preferred_element_type=f32)
            for owner in range(devices):
                part[owner % 2, owner // 2, b * each : (b + span) * each, :] = jnp.concatenate(
                    [
                        added[owner * each : (owner + 1) * each, j * LANES : (j + 1) * LANES]
                        for j in range(span)
                    ],
                    axis=0,
                )
        pl.semaphore_wait(barrier, pairs)

        def first_send(k, _):
            to_partner(far(k)).start()
            return 0

        lax.fori_loop(0, pairs - 1, first_send, 0)
        to_partner(pair).start()
        rows, more = window * each, blocks * each

        def merge(g):
            to_partner(g).wait_recv()
            own, other = part[core, g], arrived[g]
            early = jnp.where(core == 0, own, other)
            later = jnp.where(core == 0, other, own)
            middle = early[more:] + later[: rows - more]
            return early[:more], middle, later[rows - more :]

        def second_send(k, _):
            g = far(k)
            begin, middle, end = merge(g)
            merged[g, 0:more] = begin
            merged[g, more:rows] = middle
            merged[g, rows : rows + more] = end
            to_owner(k).start()
            return 0

        lax.fori_loop(0, pairs - 1, second_send, 0)
        begin, middle, end = merge(pair)
        joined[pair, 0:more] = begin
        joined[pair, more:rows] = middle
        joined[pair, rows : rows + more] = end

        for load in loads[1:]:
            load.wait()
        cosine, sine = twiddle_ref[0], twiddle_ref[1]
        values = template_ref[...]
        count = lags // LANES
        for b in range(count):
            series[b * each : (b + 1) * each, :] = values[:, b * LANES : (b + 1) * LANES]
        series[count * each :, :] = jnp.zeros(((outer - count) * each, LANES), f32)
        energy = jnp.sqrt(jnp.sum(values * values, axis=1, keepdims=True) + 1e-06)
        factor = 1.0 / (outer * LANES * math.sqrt(channels) * energy)

        def columns():
            return [series[pl.ds(k, outer, stride=each), :] for k in range(each)]

        templ = transform(columns(), first_ref, forward_ref, cosine, sine)

        def finish(k, _):
            to_owner(k).wait()
            return 0

        lax.fori_loop(0, pairs - 1, finish, 0)

        def leave(g, _):
            to_partner(g).wait_send()
            return 0

        lax.fori_loop(0, pairs, leave, 0)
        series[...] = jnp.zeros(series.shape, f32)
        local = 2 * blocks
        wide = window + blocks
        for source in range(pairs):
            for b in range(0, wide, local):
                taken = min(local, wide - b)
                block = (source * local + b - REACH // LANES) % outer
                here = slice(block * each, (block + taken) * each)
                series[here, :] = series[here, :] + joined[source, b * each : (b + taken) * each, :]
        stack = transform(columns(), first_ref, forward_ref, cosine, sine)
        stack_re, stack_im = stack[:, :LANES], stack[:, LANES:]
        templ_re, templ_im = templ[:, :LANES], templ[:, LANES:]
        product = jnp.concatenate(
            [stack_re * templ_re + stack_im * templ_im, stack_im * templ_re - stack_re * templ_im], axis=1
        )
        high, low = split(product)
        back = jnp.dot(jnp.concatenate([high, low, high], axis=1), back_ref[...], preferred_element_type=f32)
        turned = []
        for k in range(each):
            re = back[k * outer : (k + 1) * outer, :LANES]
            im = back[k * outer : (k + 1) * outer, LANES:]
            turned.append(jnp.concatenate([re * cosine - im * sine, re * sine + im * cosine], axis=0))
        high, low = split(jnp.concatenate(turned, axis=1))
        final = jnp.dot(last_ref[...], jnp.concatenate([high, high, low], axis=0), preferred_element_type=f32)
        for k in range(each):
            tail[pl.ds(k, count, stride=each), :] = final[:, k * LANES : (k + 1) * LANES]
        for b in range(count):
            out_ref[:, b * LANES : (b + 1) * LANES] = tail[b * each : (b + 1) * each, :] * factor


def tables(length, lags):
    outer = length // LANES
    turn = 2.0 * math.pi
    ramp = np.arange(outer)[:, None] * np.arange(outer)[None, :] % outer * (turn / outer)
    wide = np.arange(LANES)[:, None] * np.arange(LANES)[None, :] % LANES * (turn / LANES)
    twist = np.arange(outer)[:, None] * np.arange(LANES)[None, :] % length * (turn / length)
    first = split_table(np.concatenate([np.cos(ramp), -np.sin(ramp)], axis=0))
    cosine, sine = np.cos(wide), np.sin(wide)
    forward = split_table(np.block([[cosine, -sine], [sine, cosine]]))
    back = split_table(np.block([[cosine, sine], [-sine, cosine]]))
    shown = ramp[: lags // LANES]
    last = split_table(np.concatenate([np.cos(shown), -np.sin(shown)], axis=1))
    return (
        np.concatenate([first[0], first[1], first[0]], axis=1),
        np.concatenate([forward[0], forward[0], forward[1]], axis=0),
        np.concatenate([back[0], back[0], back[1]], axis=0),
        np.concatenate([last[0], last[1], last[0]], axis=1),
        np.stack([np.cos(twist), np.sin(twist)]).astype(np.float32),
    )


def on_device(devices, traces, templates, moveouts, masks):
    channels, width = traces.shape
    each, lags = templates.shape
    blocks = width // LANES
    outer = devices * blocks
    window = blocks + REACH // LANES
    depth = math.gcd(channels, 256)
    pairs = devices // 2
    loaded = [masks, templates, *[jnp.asarray(table) for table in tables(outer * LANES, lags)]]
    wide = (window + blocks) * each
    return pl.pallas_call(
        functools.partial(kernel, devices, channels),
        grid=(channels // depth,),
        in_specs=[
            pl.BlockSpec((1, depth), lambda i: (0, i)),
            pl.BlockSpec((depth, width), lambda i: (i, 0)),
            *[pl.BlockSpec(memory_space=pl.ANY) for _ in loaded],
        ],
        out_specs=pl.BlockSpec((each, lags), lambda i: (0, 0)),
        out_shape=jax.ShapeDtypeStruct((each, lags), f32),
        scratch_shapes=[
            *[pltpu.VMEM(value.shape, value.dtype) for value in loaded],
            pltpu.VMEM((depth, LANES), jnp.int32),
            pltpu.VMEM((2 * channels, window * LANES), bf16),
            pltpu.VMEM((2, pairs, window * each, LANES), f32),
            pltpu.VMEM((pairs, window * each, LANES), f32),
            pltpu.VMEM((pairs, wide, LANES), f32),
            pltpu.VMEM((pairs, wide, LANES), f32),
            pltpu.VMEM((outer * each, LANES), f32),
            pltpu.VMEM((lags // LANES * each, LANES), f32),
            pltpu.SemaphoreType.DMA((len(loaded),)),
            *[pltpu.SemaphoreType.DMA((pairs,)) for _ in range(4)],
        ],
        compiler_params=pltpu.CompilerParams(collective_id=0, has_side_effects=True),
        name="detect",
    )(moveouts[None, :], traces, *loaded)


def solution(mesh):
    return jax.shard_map(
        functools.partial(on_device, mesh.shape["tm"]),
        mesh=mesh,
        in_specs=(P("grp", "tm"), P("tm", None), P("grp"), P(None, "grp")),
        out_specs=P("tm", "grp"),
        check_vma=False,
    )
```

profile of v0, /device:TPU:0, one launch (start us, length us, event | category | flops | bytes accessed | tf_op | source)
XLA Modules:
  0.0 30.8 jit_solution(2316668681469269625)
XLA Ops:
  0.0 29.2 %detect.1 = f32[4,8192]{1,0:T(4,128)} custom-call(s32[1,1024]{1,0:T(1,128)} %bitcast.1, f32[1024,1024]{1,0:T(8,128)} %traces_ref.1, s32[64,1024]{1,0:T(8,128)} %mask_hbm.1, f32[4,8192]{1,0:T(4,128)} %template_hbm.1, bf16[256,384]{1,0:T(8,128)(2,1)} %constant.10.clone.first_hbm, bf16[768,256]{1,0:T(8,128)(2,1)} %constant.11.clone.forward_hbm, ...), custom_call_target="tpu_custom_call" | custom-call | tf_op jit(solution)/shard_map/detect/pallas_call | solution.py:328
  29.2 1.6 %copy.11 = f32[4,8192]{1,0:T(4,128)} copy(f32[4,8192]{1,0:T(4,128)} %detect.1) | data formatting | bytes 262144
where the time goes:
time: 31 us; the launch traced here: 30.8 us
  Pallas kernels  29.2 us (94%)
  local copies, waits for them, and re-layouts  1.57 us (5%)
    pallas_call x1, Pallas kernels, on_device(): pl.pallas_call(functools.partial(kernel, devices, channels), grid=(channe...  29.2 us
    unnamed x1, local copies, waits for them, and re-layouts  1.57 us

commit v1 on v0

--- a/solution.py
+++ b/solution.py
@@ -12,6 +12,7 @@
 f32, bf16 = jnp.float32, jnp.bfloat16
 LANES = 128
 REACH = 2048
+COARSE = 4
 
 
 def split(value):
@@ -40,7 +41,6 @@
 def shift(traces_ref, late, terms, base, group, channels):
     rows = 16
     blocks = traces_ref.shape[1] // LANES
-    window = blocks + REACH // LANES
     here = pl.ds(pl.multiple_of(group * rows, rows), rows)
     delay = late[here, :]
     lane = lax.broadcasted_iota(jnp.int32, (rows, LANES), 1)
@@ -59,7 +59,7 @@
         for b in range(blocks + 1)
     ]
     hop = 1
-    while hop < REACH // LANES:
+    while hop < COARSE:
         chosen = ((delay // LANES) & hop) != 0
         moved = [
             jnp.where(
@@ -70,7 +70,7 @@
             for b in range(len(moved) + hop)
         ]
         hop *= 2
-    for b in range(window):
+    for b in range(len(moved)):
         high, low = split(moved[b])
         column = slice(b * LANES, (b + 1) * LANES)
         terms[pl.ds(pl.multiple_of(base + group * rows, rows), rows), column] = high
@@ -81,6 +81,7 @@
     devices,
     channels,
     moveout_ref,
+    moveouts_ref,
     traces_ref,
     mask_hbm,
     template_hbm,
@@ -99,6 +100,7 @@
     twiddle_ref,
     late,
     terms,
+    raw,
     part,
     arrived,
     merged,
@@ -156,12 +158,12 @@
         row = (REACH - 1) - moveout_ref[:, piece * LANES : (piece + 1) * LANES]
         late[piece * LANES : (piece + 1) * LANES, :] = jnp.broadcast_to(row, (LANES, LANES)).T
 
-    def group_pair(i, _):
-        for k in range(2):
-            shift(traces_ref, late, terms, step * depth, 2 * i + k, channels)
+    def four_groups(i, _):
+        for k in range(4):
+            shift(traces_ref, late, terms, step * depth, 4 * i + k, channels)
         return 0
 
-    lax.fori_loop(0, depth // 32, group_pair, 0)
+    lax.fori_loop(0, depth // 64, four_groups, 0)
 
     def far(k):
         near = (k + 1) // 2
@@ -191,18 +193,33 @@
     @pl.when(step == steps - 1)
     def _():
         loads[0].wait()
-        mask = mask_ref[...].astype(f32).astype(bf16)
-        double = jnp.concatenate([mask, mask], axis=1)
+        count = mask_ref.shape[0]
+        coarse = ((REACH - 1) - moveouts_ref[...]) // (COARSE * LANES)
+        chosen = [
+            jnp.where(coarse == h, mask_ref[...], 0).astype(f32).astype(bf16)
+            for h in range(REACH // LANES // COARSE)
+        ]
+        masks = jnp.concatenate(chosen, axis=0)
+        double = jnp.concatenate([masks, masks], axis=1)
+        fine = blocks + COARSE
+        span = 2 if fine % 2 == 0 else 1
+        for b in range(0, fine, span):
+            column = slice(b * LANES, (b + span) * LANES)
+            raw[:, column] = jnp.dot(double, terms[:, column], preferred_element_type=f32)
+
+        def stacked(b):
+            hops = [h for h in range(len(chosen)) if 0 <= b - COARSE * h < fine]
+            return sum(
+                raw[h * count : (h + 1) * count, (b - COARSE * h) * LANES : (b - COARSE * h + 1) * LANES]
+                for h in hops
+            )
+
         span = 2 if window % 2 == 0 else 1
         for b in range(0, window, span):
-            added = jnp.dot(double, terms[:, b * LANES : (b + span) * LANES], preferred_element_type=f32)
+            added = [stacked(b + j) for j in range(span)]
             for owner in range(devices):
                 part[owner % 2, owner // 2, b * each : (b + span) * each, :] = jnp.concatenate(
-                    [
-                        added[owner * each : (owner + 1) * each, j * LANES : (j + 1) * LANES]
-                        for j in range(span)
-                    ],
-                    axis=0,
+                    [value[owner * each : (owner + 1) * each] for value in added], axis=0
                 )
         pl.semaphore_wait(barrier, pairs)
 
@@ -330,6 +347,7 @@
         grid=(channels // depth,),
         in_specs=[
             pl.BlockSpec((1, depth), lambda i: (0, i)),
+            pl.BlockSpec((1, channels), lambda i: (0, 0)),
             pl.BlockSpec((depth, width), lambda i: (i, 0)),
             *[pl.BlockSpec(memory_space=pl.ANY) for _ in loaded],
         ],
@@ -338,7 +356,8 @@
         scratch_shapes=[
             *[pltpu.VMEM(value.shape, value.dtype) for value in loaded],
             pltpu.VMEM((depth, LANES), jnp.int32),
-            pltpu.VMEM((2 * channels, window * LANES), bf16),
+            pltpu.VMEM((2 * channels, (blocks + COARSE) * LANES), bf16),
+            pltpu.VMEM((REACH // LANES // COARSE * masks.shape[0], (blocks + COARSE) * LANES), f32),
             pltpu.VMEM((2, pairs, window * each, LANES), f32),
             pltpu.VMEM((pairs, window * each, LANES), f32),
             pltpu.VMEM((pairs, wide, LANES), f32),
@@ -350,7 +369,7 @@
         ],
         compiler_params=pltpu.CompilerParams(collective_id=0, has_side_effects=True),
         name="detect",
-    )(moveouts[None, :], traces, *loaded)
+    )(moveouts[None, :], moveouts[None, :], traces, *loaded)
 
 
 def solution(mesh):

time: 31 us -> 28.5 us (0.919)
  Pallas kernels: 29.2 us -> 26.7 us
    pallas_call x1, Pallas kernels: 29.2 us -> 26.7 us  [on_device(): pl.pallas_call(functools.partial(kernel, devices, channels), grid=(channe...]
where the time goes in v1:
time: 28.5 us; the launch traced here: 28.3 us
  Pallas kernels  26.7 us (94%)
  local copies, waits for them, and re-layouts  1.57 us (6%)
    pallas_call x1, Pallas kernels, on_device(): pl.pallas_call(functools.partial(kernel, devices, channels), grid=(channe...  26.7 us
    unnamed x1, local copies, waits for them, and re-layouts  1.57 us

profile of v1, /device:TPU:0, one launch (start us, length us, event | category | flops | bytes accessed | tf_op | source)
XLA Modules:
  0.0 28.3 jit_solution(1319288016752372864)
XLA Ops:
  0.0 26.7 %detect.1 = f32[4,8192]{1,0:T(4,128)} custom-call(s32[1,1024]{1,0:T(1,128)} %bitcast.1, s32[1,1024]{1,0:T(1,128)} %bitcast.2, f32[1024,1024]{1,0:T(8,128)} %traces_ref.1, s32[64,1024]{1,0:T(8,128)} %mask_hbm.1, f32[4,8192]{1,0:T(4,128)} %template_hbm.1, bf16[256,384]{1,0:T(8,128)(2,1)} %constant.10.clone.first_hbm, ...), custom_call_target="tpu_custom_call" | custom-call | tf_op jit(solution)/shard_map/detect/pallas_call | solution.py:345
  26.7 1.6 %copy.11 = f32[4,8192]{1,0:T(4,128)} copy(f32[4,8192]{1,0:T(4,128)} %detect.1) | data formatting | bytes 262144

commit v2 on v1

--- a/solution.py
+++ b/solution.py
@@ -165,9 +165,12 @@
 
     lax.fori_loop(0, depth // 64, four_groups, 0)
 
-    def far(k):
-        near = (k + 1) // 2
-        return lax.rem(pair + pairs // 2 + near * (1 - 2 * lax.rem(k, 2)), pairs)
+    middle_of = pairs // 2
+    own_half = pair // middle_of
+
+    def peer(stage, j):
+        half = own_half if stage else 1 - own_half
+        return half * middle_of + lax.rem(pair + j, middle_of)
 
     def to_partner(g):
         return pltpu.make_async_remote_copy(
@@ -179,8 +182,9 @@
             device_id_type=pl.DeviceIdType.MESH,
         )
 
-    def to_owner(k):
-        g = far(k)
+    def to_owner(stage, j):
+        g = peer(stage, j)
+        k = j + stage * (middle_of - 1)
         return pltpu.make_async_remote_copy(
             src_ref=merged.at[g],
             dst_ref=joined.at[pair],
@@ -193,41 +197,48 @@
     @pl.when(step == steps - 1)
     def _():
         loads[0].wait()
-        count = mask_ref.shape[0]
+        count = mask_ref.shape[0] // 2
         coarse = ((REACH - 1) - moveouts_ref[...]) // (COARSE * LANES)
-        chosen = [
-            jnp.where(coarse == h, mask_ref[...], 0).astype(f32).astype(bf16)
-            for h in range(REACH // LANES // COARSE)
-        ]
-        masks = jnp.concatenate(chosen, axis=0)
-        double = jnp.concatenate([masks, masks], axis=1)
+        hops = REACH // LANES // COARSE
         fine = blocks + COARSE
-        span = 2 if fine % 2 == 0 else 1
-        for b in range(0, fine, span):
-            column = slice(b * LANES, (b + span) * LANES)
-            raw[:, column] = jnp.dot(double, terms[:, column], preferred_element_type=f32)
-
-        def stacked(b):
-            hops = [h for h in range(len(chosen)) if 0 <= b - COARSE * h < fine]
-            return sum(
-                raw[h * count : (h + 1) * count, (b - COARSE * h) * LANES : (b - COARSE * h + 1) * LANES]
-                for h in hops
-            )
-
-        span = 2 if window % 2 == 0 else 1
-        for b in range(0, window, span):
-            added = [stacked(b + j) for j in range(span)]
-            for owner in range(devices):
-                part[owner % 2, owner // 2, b * each : (b + span) * each, :] = jnp.concatenate(
-                    [value[owner * each : (owner + 1) * each] for value in added], axis=0
+
+        def stacks(half):
+            held = mask_ref[pl.ds(pl.multiple_of(half * count, 8), count), :]
+            chosen = [jnp.where(coarse == h, held, 0).astype(f32).astype(bf16) for h in range(hops)]
+            masks = jnp.concatenate(chosen, axis=0)
+            double = jnp.concatenate([masks, masks], axis=1)
+            span = 2 if fine % 2 == 0 else 1
+            for b in range(0, fine, span):
+                column = slice(b * LANES, (b + span) * LANES)
+                raw[:, column] = jnp.dot(double, terms[:, column], preferred_element_type=f32)
+
+            def stacked(b):
+                return sum(
+                    raw[h * count : (h + 1) * count, (b - COARSE * h) * LANES : (b - COARSE * h + 1) * LANES]
+                    for h in range(hops)
+                    if 0 <= b - COARSE * h < fine
                 )
+
+            span = 2 if window % 2 == 0 else 1
+            for b in range(0, window, span):
+                added = [stacked(b + j) for j in range(span)]
+                for owner in range(pairs):
+                    part[owner % 2, half * middle_of + owner // 2, b * each : (b + span) * each, :] = (
+                        jnp.concatenate([value[owner * each : (owner + 1) * each] for value in added], axis=0)
+                    )
+
+        def first_sends(stage):
+            def start(j, _):
+                to_partner(peer(stage, j)).start()
+                return 0
+
+            lax.fori_loop(stage, middle_of, start, 0)
+
+        stacks(1 - own_half)
         pl.semaphore_wait(barrier, pairs)
-
-        def first_send(k, _):
-            to_partner(far(k)).start()
-            return 0
-
-        lax.fori_loop(0, pairs - 1, first_send, 0)
+        first_sends(0)
+        stacks(own_half)
+        first_sends(1)
         to_partner(pair).start()
         rows, more = window * each, blocks * each
 
@@ -239,16 +250,20 @@
             middle = early[more:] + later[: rows - more]
             return early[:more], middle, later[rows - more :]
 
-        def second_send(k, _):
-            g = far(k)
-            begin, middle, end = merge(g)
-            merged[g, 0:more] = begin
-            merged[g, more:rows] = middle
-            merged[g, rows : rows + more] = end
-            to_owner(k).start()
-            return 0
-
-        lax.fori_loop(0, pairs - 1, second_send, 0)
+        def second_sends(stage):
+            def start(j, _):
+                g = peer(stage, j)
+                begin, middle, end = merge(g)
+                merged[g, 0:more] = begin
+                merged[g, more:rows] = middle
+                merged[g, rows : rows + more] = end
+                to_owner(stage, j).start()
+                return 0
+
+            lax.fori_loop(stage, middle_of, start, 0)
+
+        second_sends(0)
+        second_sends(1)
         begin, middle, end = merge(pair)
         joined[pair, 0:more] = begin
         joined[pair, more:rows] = middle
@@ -270,11 +285,15 @@
 
         templ = transform(columns(), first_ref, forward_ref, cosine, sine)
 
-        def finish(k, _):
-            to_owner(k).wait()
-            return 0
-
-        lax.fori_loop(0, pairs - 1, finish, 0)
+        def finish(stage):
+            def wait(j, _):
+                to_owner(stage, j).wait()
+                return 0
+
+            lax.fori_loop(stage, middle_of, wait, 0)
+
+        finish(1)
+        finish(0)
 
         def leave(g, _):
             to_partner(g).wait_send()
@@ -357,7 +376,7 @@
             *[pltpu.VMEM(value.shape, value.dtype) for value in loaded],
             pltpu.VMEM((depth, LANES), jnp.int32),
             pltpu.VMEM((2 * channels, (blocks + COARSE) * LANES), bf16),
-            pltpu.VMEM((REACH // LANES // COARSE * masks.shape[0], (blocks + COARSE) * LANES), f32),
+            pltpu.VMEM((REACH // LANES // COARSE * masks.shape[0] // 2, (blocks + COARSE) * LANES), f32),
             pltpu.VMEM((2, pairs, window * each, LANES), f32),
             pltpu.VMEM((pairs, window * each, LANES), f32),
             pltpu.VMEM((pairs, wide, LANES), f32),

time: 28.5 us -> 29.3 us (1.028)
  Pallas kernels: 26.7 us -> 27.5 us
    pallas_call x1, Pallas kernels: 26.7 us -> 27.5 us  [on_device(): pl.pallas_call(functools.partial(kernel, devices, channels), grid=(channe...]
where the time goes in v2:
time: 29.3 us; the launch traced here: 29.1 us
  Pallas kernels  27.5 us (94%)
  local copies, waits for them, and re-layouts  1.57 us (5%)
    pallas_call x1, Pallas kernels, on_device(): pl.pallas_call(functools.partial(kernel, devices, channels), grid=(channe...  27.5 us
    unnamed x1, local copies, waits for them, and re-layouts  1.57 us

profile of v2, /device:TPU:0, one launch (start us, length us, event | category | flops | bytes accessed | tf_op | source)
XLA Modules:
  0.0 29.1 jit_solution(13944597239144922985)
XLA Ops:
  0.0 27.5 %detect.1 = f32[4,8192]{1,0:T(4,128)} custom-call(s32[1,1024]{1,0:T(1,128)} %bitcast.1, s32[1,1024]{1,0:T(1,128)} %bitcast.2, f32[1024,1024]{1,0:T(8,128)} %traces_ref.1, s32[64,1024]{1,0:T(8,128)} %mask_hbm.1, f32[4,8192]{1,0:T(4,128)} %template_hbm.1, bf16[256,384]{1,0:T(8,128)(2,1)} %constant.10.clone.first_hbm, ...), custom_call_target="tpu_custom_call" | custom-call | tf_op jit(solution)/shard_map/detect/pallas_call | solution.py:364
  27.5 1.6 %copy.11 = f32[4,8192]{1,0:T(4,128)} copy(f32[4,8192]{1,0:T(4,128)} %detect.1) | data formatting | bytes 262144

commit v3 on v1

--- a/solution.py
+++ b/solution.py
@@ -165,9 +165,8 @@
 
     lax.fori_loop(0, depth // 64, four_groups, 0)
 
-    def far(k):
-        near = (k + 1) // 2
-        return lax.rem(pair + pairs // 2 + near * (1 - 2 * lax.rem(k, 2)), pairs)
+    def peer(k):
+        return lax.rem(pair + 1 + k, pairs)
 
     def to_partner(g):
         return pltpu.make_async_remote_copy(
@@ -180,7 +179,7 @@
         )
 
     def to_owner(k):
-        g = far(k)
+        g = peer(k)
         return pltpu.make_async_remote_copy(
             src_ref=merged.at[g],
             dst_ref=joined.at[pair],
@@ -224,7 +223,7 @@
         pl.semaphore_wait(barrier, pairs)
 
         def first_send(k, _):
-            to_partner(far(k)).start()
+            to_partner(peer(k)).start()
             return 0
 
         lax.fori_loop(0, pairs - 1, first_send, 0)
@@ -240,7 +239,7 @@
             return early[:more], middle, later[rows - more :]
 
         def second_send(k, _):
-            g = far(k)
+            g = peer(k)
             begin, middle, end = merge(g)
             merged[g, 0:more] = begin
             merged[g, more:rows] = middle

time: 28.5 us -> 27.1 us (0.951)
  the two profiles are of different devices: /device:TPU:0 before, /device:TPU:11 now
where the time goes in v3:
time: 27.1 us; the launch traced here: 27 us
  Pallas kernels  25.4 us (94%)
  local copies, waits for them, and re-layouts  1.57 us (6%)
    pallas_call x1, Pallas kernels, on_device(): pl.pallas_call(functools.partial(kernel, devices, channels), grid=(channe...  25.4 us
    unnamed x1, local copies, waits for them, and re-layouts  1.57 us

profile of v3, /device:TPU:11, one launch (start us, length us, event | category | flops | bytes accessed | tf_op | source)
XLA Modules:
  0.0 27.0 jit_solution(6212534600668766674)
XLA Ops:
  0.0 25.4 %detect.1 = f32[4,8192]{1,0:T(4,128)} custom-call(s32[1,1024]{1,0:T(1,128)} %bitcast.1, s32[1,1024]{1,0:T(1,128)} %bitcast.2, f32[1024,1024]{1,0:T(8,128)} %traces_ref.1, s32[64,1024]{1,0:T(8,128)} %mask_hbm.1, f32[4,8192]{1,0:T(4,128)} %template_hbm.1, bf16[256,384]{1,0:T(8,128)(2,1)} %constant.10.clone.first_hbm, ...), custom_call_target="tpu_custom_call" | custom-call | tf_op jit(solution)/shard_map/detect/pallas_call | solution.py:344
  25.4 1.6 %copy.11 = f32[4,8192]{1,0:T(4,128)} copy(f32[4,8192]{1,0:T(4,128)} %detect.1) | data formatting | bytes 262144
